TPU v7x, 8 devices: a whole 2x2x1 slice. The times are simulated.
8 devices in a mesh: z: 2 (over z, y), y: 2 (over x), x: 2 (over core).
Axes of the slice: x: 2, y: 2, z: 1, core: 2. Of those that a mesh axis runs over, the one named last changes fastest.
Arguments:
- atom_pos: float32 [5832, 3], P(('z', 'y', 'x'))
- atom_vel: float32 [5832, 3], P(('z', 'y', 'x'))
- atom_frc: float32 [5832, 3], P(('z', 'y', 'x'))
- atom_id: int32 [5832], P(('z', 'y', 'x'))
- atom_ok: int32 [5832], P(('z', 'y', 'x'))
- brick_side: float32 [], replicated
Outputs:
- output 1: float32 [5832, 3], P(('z', 'y', 'x'))
- output 2: float32 [5832, 3], P(('z', 'y', 'x'))
- output 3: float32 [5832, 3], P(('z', 'y', 'x'))
- output 4: int32 [5832], P(('z', 'y', 'x'))
- output 5: int32 [5832], P(('z', 'y', 'x'))
- output 6: float32 [], replicated
All inputs are finite; a program needn't handle non-finite values.
Results may differ from a plain program's by a relative error of at most 0.001.
Values sent between devices are 32-bit elements.
A program may use at most 1 GiB of HBM per device.

v0:
```python
import functools

import jax
import jax.numpy as jnp
from jax import lax
from jax.experimental import pallas as pl
from jax.experimental.pallas import tpu as pltpu
from jax.sharding import PartitionSpec as P

DT = 0.005
RC = 2.5
FAR_AWAY = 1.0e6
UCUT = 4.0 * (RC ** -12 - RC ** -6)
UPC = -48.0 * RC ** -13 + 24.0 * RC ** -7
MESH_AXES = ("z", "y", "x")
CAP = 729
PAD = 768
MIG = 256
FULL = PAD + MIG
SEG = {1: (0, 16), 2: (16, 16), 4: (32, 16), 3: (48, 32), 5: (80, 32), 6: (128, 32), 7: (160, 64)}
IC = 32
FAR_FIRST = (6, 7, 4, 2, 5, 3, 1)
REACH = RC + 0.01
MESH_ID = pl.DeviceIdType.MESH


def pieces_of(rows):
    first = rows.astype(jnp.bfloat16).astype(jnp.float32)
    rest = rows - first
    second = rest.astype(jnp.bfloat16).astype(jnp.float32)
    third = rest - second
    return jnp.concatenate([first, second, third], axis=0).astype(jnp.bfloat16)


def select_rows(rows, onehot):
    out = lax.dot_general(pieces_of(rows), onehot, (((1,), (1,)), ((), ())), preferred_element_type=jnp.float32)
    return out[0:8] + out[8:16] + out[16:24]


def partner(relation):
    mine = (lax.axis_index("z"), lax.axis_index("y"), lax.axis_index("x"))
    bits = (relation // 4 % 2, relation // 2 % 2, relation % 2)
    return tuple((axis + bit) % 2 for axis, bit in zip(mine, bits))


def greet():
    barrier = pltpu.get_barrier_semaphore()
    for relation in range(1, 8):
        pl.semaphore_signal(barrier, inc=1, device_id=partner(relation), device_id_type=MESH_ID)
    return barrier


def axis_column(values, rows):
    idx = lax.broadcasted_iota(jnp.int32, (rows, 1), 0)
    out = jnp.full((rows, 1), values[-1], jnp.float32)
    for k in range(len(values) - 1):
        out = jnp.where(idx == k, values[k], out)
    return out


def brick_coords():
    return [lax.axis_index(name).astype(jnp.float32) for name in ("x", "y", "z")]


def prefix_counts(member):
    blocks = PAD // 128
    stacked = jnp.concatenate([member[:, 128 * b:128 * (b + 1)] for b in range(blocks)], axis=0).astype(jnp.bfloat16)
    row = lax.broadcasted_iota(jnp.int32, (128, 256), 0)
    col = lax.broadcasted_iota(jnp.int32, (128, 256), 1)
    ladder = ((row < col) | (col >= 128)).astype(jnp.float32).astype(jnp.bfloat16)
    counts = jnp.dot(stacked, ladder, preferred_element_type=jnp.float32)
    before = jnp.zeros((8, 128), jnp.float32)
    ranks = []
    for b in range(blocks):
        ranks.append(counts[8 * b:8 * b + 8, 0:128] + before)
        before = before + counts[8 * b:8 * b + 8, 128:256]
    return jnp.concatenate(ranks, axis=1), before


def exchange_kernel(pos_hbm, vel_hbm, frc_hbm, id_hbm, ok_hbm, side_ref, own_ref, all_ref, mig_ref, pos_ref, vel_ref, frc_ref, id_ref, ok_ref, pad_ref, load_sem, send_sem, recv_sem):
    loads = []
    for k, (src, dst) in enumerate(((pos_hbm, pos_ref), (vel_hbm, vel_ref), (frc_hbm, frc_ref), (id_hbm, id_ref), (ok_hbm, ok_ref))):
        load = pltpu.make_async_copy(src, dst, load_sem.at[k])
        load.start()
        loads.append(load)
    barrier = greet()
    side = side_ref[0, 0]
    box = side * 2.0
    pad_ref[...] = jnp.zeros_like(pad_ref)
    for load in loads:
        load.wait()
    half_v = vel_ref[...] + (0.5 * DT) * frc_ref[...]
    pad_ref[0:3, 0:CAP] = pos_ref[...] + DT * half_v
    pad_ref[3:6, 0:CAP] = half_v
    pad_ref[6:7, 0:CAP] = (id_ref[...].reshape(1, CAP) >> 16).astype(jnp.float32) + 1.0
    pad_ref[7:8, 0:CAP] = (id_ref[...].reshape(1, CAP) & 65535).astype(jnp.float32)
    pad_ref[8:9, 0:CAP] = ok_ref[...].reshape(1, CAP).astype(jnp.float32)
    unwrapped = pad_ref[0:3, :]
    owned = pad_ref[8:9, :] > 0.5
    moved = jnp.where(unwrapped < 0.0, unwrapped + box, jnp.where(unwrapped >= box, unwrapped - box, unwrapped))
    for axis in range(3):
        all_ref[0, :, PAD * axis:PAD * (axis + 1)] = jnp.where(owned, moved[axis:axis + 1, :], FAR_AWAY)

    low = axis_column([coord * side for coord in brick_coords()], 3)
    outside = (unwrapped < low) | (unwrapped >= low + side)
    bits = jnp.where(outside, axis_column([1.0, 2.0, 4.0], 3), 0.0)
    code = jnp.sum(bits, axis=0, keepdims=True)
    code = jnp.where(owned, code, -1.0)
    relation_col = lax.broadcasted_iota(jnp.int32, (8, PAD), 0).astype(jnp.float32)
    member = code == relation_col
    rank, _ = prefix_counts(member.astype(jnp.float32))
    offset = axis_column([0.0] + [float(SEG[m][0]) for m in range(1, 8)], 8)
    slot = jnp.sum(jnp.where(member, rank + offset, 0.0), axis=0, keepdims=True)
    slot = jnp.where(code > 0.5, slot, -1.0)
    rows = jnp.concatenate([moved, pad_ref[3:8, :]], axis=0)
    slots = lax.broadcasted_iota(jnp.int32, (MIG, PAD), 0).astype(jnp.float32)
    onehot = (slots == slot).astype(jnp.float32).astype(jnp.bfloat16)
    mig_ref[0] = select_rows(rows, onehot)
    own_ref[0:8, :] = rows
    own_ref[8:9, :] = jnp.where(code == 0.0, rank[0:1, :], -1.0)

    pl.semaphore_wait(barrier, 7)
    copies = []
    for relation in FAR_FIRST:
        block = pl.ds(SEG[relation][0] // 128 * 128, 128)
        for which, src, dst in ((0, mig_ref.at[0, :, block], mig_ref.at[relation, :, block]), (1, all_ref.at[0], all_ref.at[relation])):
            copy = pltpu.make_async_remote_copy(src_ref=src, dst_ref=dst, send_sem=send_sem.at[which, relation], recv_sem=recv_sem.at[which, relation], device_id=partner(relation), device_id_type=MESH_ID)
            copy.start()
            copies.append(copy)
    for copy in copies:
        copy.wait()


def pair_terms(own, other, span):
    delta = []
    for mine, theirs in zip(own, other):
        diff = mine - theirs
        if span is not None:
            diff = diff - jnp.where(diff > 0.5 * span, span, jnp.where(diff < -0.5 * span, -span, 0.0))
        delta.append(diff)
    dist_sq = delta[0] * delta[0] + delta[1] * delta[1] + delta[2] * delta[2]
    in_range = (dist_sq < RC * RC) & (dist_sq > 0.01)
    inv_r = jnp.where(in_range, lax.rsqrt(dist_sq), 0.0)
    inv_r2 = inv_r * inv_r
    inv_r6 = inv_r2 * inv_r2 * inv_r2
    inv_r12 = inv_r6 * inv_r6
    well = inv_r12 - inv_r6
    scale = (well + inv_r12) * inv_r2 + (UPC / 24.0) * inv_r
    return [scale * d for d in delta], [well, dist_sq * inv_r, jnp.where(in_range, 1.0, 0.0)]


def force_kernel(own_ref, all_ref, mig_ref, side_ref, pos_ref, vel_ref, frc_ref, id_ref, ok_ref, en_ref, cand_ref, near_ref, mine_ref, acc_ref, plane_ref, list_ref):
    side = side_ref[0, 0]
    box = side * 2.0
    lane = lax.broadcasted_iota(jnp.int32, (1, MIG), 1)
    arrivals = jnp.zeros((8, MIG), jnp.float32)
    for relation, (start, size) in SEG.items():
        arrivals = jnp.where((lane >= start) & (lane < start + size), mig_ref[relation], arrivals)
    cand_ref[:, 0:PAD] = own_ref[0:8, :]
    cand_ref[:, PAD:FULL] = arrivals
    stay_rank = own_ref[8:9, :]
    cand = cand_ref[...]
    valid = jnp.concatenate([stay_rank >= 0.0, arrivals[6:7, :] > 0.5], axis=1)
    number = (cand[6:7, :].astype(jnp.int32) - 1) * 65536 + cand[7:8, :].astype(jnp.int32)
    key = jnp.where(valid, number, 2147483647)
    total = jnp.sum(valid.astype(jnp.int32))
    key_col = jnp.transpose(jnp.broadcast_to(key[:, PAD:FULL], (8, MIG)))[:, 0:1]
    below = (key_col < key).astype(jnp.float32).astype(jnp.bfloat16)
    in_front = jnp.dot(jnp.ones((8, MIG), jnp.bfloat16), below, preferred_element_type=jnp.float32)[0:1, :]
    above = lax.dot_general(jnp.ones((8, PAD), jnp.bfloat16), below[:, 0:PAD], (((1,), (1,)), ((), ())), preferred_element_type=jnp.float32)[0:1, :]
    rank = in_front + jnp.concatenate([stay_rank, float(PAD) - above], axis=1)
    rank = jnp.where(valid, rank, -1.0)
    slots = lax.broadcasted_iota(jnp.int32, (PAD, FULL), 0).astype(jnp.float32)
    onehot = (slots == rank).astype(jnp.float32).astype(jnp.bfloat16)
    rows = select_rows(cand, onehot)
    filled = rows[6:7, :] > 0.5

    centre = [(coord + 0.5) * side for coord in brick_coords()]
    local = rows[0:3, :] - axis_column(centre, 3)
    near_ref[0:3, 0:PAD] = jnp.where(filled, local, FAR_AWAY)
    local = jnp.concatenate([jnp.where(filled, local, -FAR_AWAY), jnp.zeros((5, PAD), jnp.float32)], axis=0)
    piece_row = lax.broadcasted_iota(jnp.int32, (24, 384), 0) % 8
    piece_col = lax.broadcasted_iota(jnp.int32, (24, 384), 1) // 128
    spread = (piece_row == piece_col).astype(jnp.float32).astype(jnp.bfloat16)
    columns = lax.dot_general(pieces_of(local), spread, (((0,), (0,)), ((), ())), preferred_element_type=jnp.float32)
    for axis in range(3):
        mine_ref[axis] = columns[:, 128 * axis:128 * axis + 128]
    for relation in range(8):
        for axis in range(3):
            plane_ref[axis, relation:relation + 1, :] = all_ref[relation, :, PAD * axis:PAD * (axis + 1)]
    planes = []
    beyond = jnp.zeros((8, PAD), jnp.float32)
    for axis in range(3):
        theirs = plane_ref[axis] - centre[axis]
        theirs = jnp.where(theirs > side, theirs - box, jnp.where(theirs < -side, theirs + box, theirs))
        excess = jnp.maximum(jnp.abs(theirs) - 0.5 * side, 0.0)
        beyond = beyond + excess * excess
        planes.append(theirs)
    keep = (beyond < REACH * REACH) & (beyond > 0.0)
    front, held = prefix_counts(keep.astype(jnp.float32))
    lane8 = lax.broadcasted_iota(jnp.int32, (8, PAD), 1)
    hops = jnp.where(keep, lane8 - front.astype(jnp.int32), 0)
    for bit in range(10):
        step = 1 << bit
        coming = pltpu.roll(hops, PAD - step, 1)
        take = (coming & step) != 0
        leave = (hops & step) != 0
        hops = jnp.where(take, coming, jnp.where(leave, 0, hops))
        planes = [jnp.where(take, pltpu.roll(plane, PAD - step, 1), plane) for plane in planes]
    for relation in range(8):
        for axis in range(3):
            list_ref[relation, axis:axis + 1, 0:PAD] = planes[axis][relation:relation + 1, :]
    held = held.astype(jnp.int32)
    lane128 = lax.broadcasted_iota(jnp.int32, (8, 128), 1)
    start = total
    for relation in range(8):
        into = start % 128
        first = pl.multiple_of(start - into, 128)
        turned = pltpu.roll(list_ref[relation], into, 1)
        near_ref[:, pl.ds(first, 128)] = jnp.where(lane128 < into, near_ref[:, pl.ds(first, 128)], turned[:, 0:128])
        near_ref[:, pl.ds(pl.multiple_of(first + 128, 128), PAD)] = turned[:, 128:PAD + 128]
        start = start + held[relation, 0]
    into = start % 128
    first = pl.multiple_of(start - into, 128)
    near_ref[:, pl.ds(first, 128)] = jnp.where(lane128 < into, near_ref[:, pl.ds(first, 128)], FAR_AWAY)
    near_ref[:, pl.ds(pl.multiple_of(first + 128, 128), 256)] = jnp.full((8, 256), FAR_AWAY, jnp.float32)
    n_other = (start + 255) // 256
    n_own = (total + IC - 1) // IC

    def sweep(span):
        def own_step(i, totals):
            first = pl.multiple_of(i * IC, IC)
            own = [mine_ref[axis, pl.ds(first, IC), :] for axis in range(3)]

            def other_step(j, sums):
                forces, totals = sums
                lanes = pl.multiple_of(j * 256, 256)
                for half in range(2):
                    other = [near_ref[axis:axis + 1, pl.ds(lanes + 128 * half, 128)] for axis in range(3)]
                    force, parts = pair_terms(own, other, span)
                    forces = tuple(f + t for f, t in zip(forces, force))
                    totals = tuple(t + ((p[0:8] + p[8:16]) + (p[16:24] + p[24:32])) for t, p in zip(totals, parts))
                return forces, totals

            zero = jnp.zeros((IC, 128), jnp.float32)
            forces, totals = lax.fori_loop(0, n_other, other_step, ((zero,) * 3, totals))
            for axis in range(3):
                acc_ref[axis, pl.ds(first, IC), :] = forces[axis]
            return totals

        zero = jnp.zeros((8, 128), jnp.float32)
        well, distance, pairs = lax.fori_loop(0, n_own, own_step, (zero,) * 3)
        energy = 4.0 * well - UPC * distance - (UCUT - RC * UPC) * pairs
        en_ref[...] = jnp.sum(energy, axis=0, keepdims=True)

    @pl.when(side >= 2.0 * RC)
    def _():
        sweep(None)

    @pl.when(side < 2.0 * RC)
    def _():
        sweep(box)

    out_rows = []
    for axis in range(3):
        parts = []
        for b in range(PAD // 128):
            parts.append(jnp.sum(jnp.transpose(acc_ref[axis, 128 * b:128 * b + 128, :]), axis=0, keepdims=True))
        out_rows.append(jnp.concatenate(parts, axis=1))
    force = jnp.where(filled, 24.0 * jnp.concatenate(out_rows, axis=0), 0.0)
    frc_ref[...] = force[:, 0:CAP]
    pos_ref[...] = rows[0:3, 0:CAP]
    vel_ref[...] = (rows[3:6, :] + (0.5 * DT) * force)[:, 0:CAP]
    new_id = (rows[6:7, :].astype(jnp.int32) - 1) * 65536 + rows[7:8, :].astype(jnp.int32)
    id_ref[...] = jnp.where(filled, new_id, 0)[:, 0:CAP].reshape(CAP)
    ok_ref[...] = filled.astype(jnp.int32)[:, 0:CAP].reshape(CAP)


def energy_kernel(en_ref, out_ref, parts_ref, send_sem, recv_sem):
    barrier = greet()
    pl.semaphore_wait(barrier, 7)
    copies = []
    for relation in FAR_FIRST:
        copy = pltpu.make_async_remote_copy(src_ref=en_ref, dst_ref=parts_ref.at[relation], send_sem=send_sem.at[relation], recv_sem=recv_sem.at[relation], device_id=partner(relation), device_id_type=MESH_ID)
        copy.start()
        copies.append(copy)
    for copy in copies:
        copy.wait()
    parts_ref[0] = en_ref[...]
    over_x = [parts_ref[k] + parts_ref[k + 1] for k in (0, 2, 4, 6)]
    total = (over_x[0] + over_x[1]) + (over_x[2] + over_x[3])
    out_ref[...] = jnp.full((1, 1), 0.5 * jnp.sum(total), jnp.float32)


def solution(mesh):
    vmem = pl.BlockSpec(memory_space=pltpu.VMEM)
    hbm = pl.BlockSpec(memory_space=pltpu.HBM)
    smem = pl.BlockSpec(memory_space=pltpu.SMEM)
    f32, i32 = jnp.float32, jnp.int32

    def shape(dims, dtype=f32):
        return jax.ShapeDtypeStruct(dims, dtype)

    exchange = pl.pallas_call(
        exchange_kernel,
        out_shape=(shape((9, PAD)), shape((8, 1, 3 * PAD)), shape((8, 8, MIG))),
        in_specs=[hbm] * 5 + [smem],
        out_specs=(vmem, vmem, vmem),
        scratch_shapes=[pltpu.VMEM((3, CAP), f32)] * 3 + [pltpu.VMEM((CAP,), i32)] * 2 + [pltpu.VMEM((9, PAD), f32), pltpu.SemaphoreType.DMA((5,)), pltpu.SemaphoreType.DMA((2, 8)), pltpu.SemaphoreType.DMA((2, 8))],
        compiler_params=pltpu.CompilerParams(collective_id=0, has_side_effects=True, vmem_limit_bytes=16 << 20),
        name="exchange",
    )
    forces = pl.pallas_call(
        force_kernel,
        out_shape=(shape((3, CAP)), shape((3, CAP)), shape((3, CAP)), shape((CAP,), i32), shape((CAP,), i32), shape((1, 128))),
        in_specs=[vmem] * 3 + [smem],
        out_specs=(vmem,) * 6,
        scratch_shapes=[pltpu.VMEM((8, FULL), f32), pltpu.VMEM((8, 9 * PAD + 256), f32), pltpu.VMEM((3, PAD, 128), f32), pltpu.VMEM((3, PAD, 128), f32), pltpu.VMEM((3, 8, PAD), f32), pltpu.VMEM((8, 8, PAD + 128), f32)],
        compiler_params=pltpu.CompilerParams(vmem_limit_bytes=16 << 20),
        name="forces",
    )
    total_energy = pl.pallas_call(
        energy_kernel,
        out_shape=shape((1, 1)),
        in_specs=[vmem],
        out_specs=vmem,
        scratch_shapes=[pltpu.VMEM((8, 1, 128), f32), pltpu.SemaphoreType.DMA((8,)), pltpu.SemaphoreType.DMA((8,))],
        compiler_params=pltpu.CompilerParams(collective_id=1, has_side_effects=True, vmem_limit_bytes=16 << 20),
        name="energy",
    )

    def local_step(atom_pos, atom_vel, atom_frc, atom_id, atom_ok, brick_side):
        side = brick_side.reshape(1, 1)
        own, everyone, movers = exchange(*[pltpu.with_memory_space_constraint(a, pltpu.HBM) for a in (atom_pos.T, atom_vel.T, atom_frc.T, atom_id, atom_ok)], side)
        pos, vel, frc, new_id, new_ok, partial = forces(own, everyone, movers, side)
        energy = total_energy(partial)
        return pos.T, vel.T, frc.T, new_id, new_ok, energy.reshape(())

    row_spec = P(MESH_AXES, None)
    id_spec = P(MESH_AXES)
    return jax.shard_map(local_step, mesh=mesh, in_specs=(row_spec, row_spec, row_spec, id_spec, id_spec, P()), out_specs=(row_spec, row_spec, row_spec, id_spec, id_spec, P()), check_vma=False)
```

profile of v0, /device:TPU:0, one launch (start us, length us, event | category | flops | bytes accessed | tf_op | source)
XLA Modules:
  0.0 23.1 jit_solution(16973430859822256368)
XLA Ops:
  1.3 7.5 %exchange.1 = (f32[9,768]{1,0:T(8,128)S(1)}, f32[8,1,2304]{2,1,0:T(1,128)S(1)}, f32[8,8,256]{2,1,0:T(8,128)S(1)}) custom-call(f32[3,729]{1,0:T(4,128)} %bitcast.10, f32[3,729]{1,0:T(4,128)} %bitcast.11, f32[3,729]{1,0:T(4,128)} %bitcast.12, s32[729]{0:T(1024)} %id_hbm.1, s32[729]{0:T(1024)} %ok_hbm.1, f32[1,1]{1,0:T(1,128)} %bitcast.8.side_ref), custom_call_target="tpu_custom_call" | custom-call | tf_op jit(solution)/shard_map/exchange/pallas_call | solution.py:334
  8.8 7.2 %forces.1 = (f32[3,729]{1,0:T(4,128)}, f32[3,729]{1,0:T(4,128)}, f32[3,729]{1,0:T(4,128)}, s32[729]{0:T(1024)}, s32[729]{0:T(1024)}, /*index=5*/f32[1,128]{1,0:T(1,128)S(1)}) custom-call(f32[9,768]{1,0:T(8,128)S(1)} %get-tuple-element.15.own_ref, f32[8,1,2304]{2,1,0:T(1,128)S(1)} %get-tuple-element.16.all_ref, f32[8,8,256]{2,1,0:T(8,128)S(1)} %get-tuple-element.17.mig_ref, ...), custom_call_target="tpu_custom_call" | custom-call | tf_op jit(solution)/shard_map/forces/pallas_call | solution.py:335
  16.1 5.3 %energy.1 = f32[1,1]{1,0:T(1,128)} custom-call(f32[1,128]{1,0:T(1,128)S(1)} %get-tuple-element.23.en_ref), custom_call_target="tpu_custom_call" | custom-call | tf_op jit(solution)/shard_map/energy/pallas_call | solution.py:336
where the time goes:
time: 23.2 us; the launch traced here: 23.1 us
  Pallas kernels  20.1 us (87%)
  between operations  3.05 us (13%)
    pallas_call x1, Pallas kernels, local_step(): exchange(*[pltpu.with_memory_space_constraint(a, pltpu.HBM) for a in (ato...  7.54 us
    pallas_call x1, Pallas kernels, local_step(): pos, vel, frc, new_id, new_ok, partial = forces(own, everyone, movers, side)  7.24 us
    pallas_call x1, Pallas kernels, local_step(): energy = total_energy(partial)  5.3 us

commit v1 on v0

--- a/solution.py
+++ b/solution.py
@@ -77,18 +77,18 @@
     return jnp.concatenate(ranks, axis=1), before
 
 
-def exchange_kernel(pos_hbm, vel_hbm, frc_hbm, id_hbm, ok_hbm, side_ref, own_ref, all_ref, mig_ref, pos_ref, vel_ref, frc_ref, id_ref, ok_ref, pad_ref, load_sem, send_sem, recv_sem):
+def exchange_kernel(pos_hbm, vel_hbm, frc_hbm, id_hbm, ok_hbm, side_hbm, own_ref, all_ref, mig_ref, pos_ref, vel_ref, frc_ref, id_ref, ok_ref, side_ref, pad_ref, load_sem, send_sem, recv_sem):
     loads = []
-    for k, (src, dst) in enumerate(((pos_hbm, pos_ref), (vel_hbm, vel_ref), (frc_hbm, frc_ref), (id_hbm, id_ref), (ok_hbm, ok_ref))):
+    for k, (src, dst) in enumerate(((pos_hbm, pos_ref), (vel_hbm, vel_ref), (frc_hbm, frc_ref), (id_hbm, id_ref), (ok_hbm, ok_ref), (side_hbm, side_ref))):
         load = pltpu.make_async_copy(src, dst, load_sem.at[k])
         load.start()
         loads.append(load)
     barrier = greet()
-    side = side_ref[0, 0]
-    box = side * 2.0
     pad_ref[...] = jnp.zeros_like(pad_ref)
     for load in loads:
         load.wait()
+    side = side_ref[...]
+    box = side * 2.0
     half_v = vel_ref[...] + (0.5 * DT) * frc_ref[...]
     pad_ref[0:3, 0:CAP] = pos_ref[...] + DT * half_v
     pad_ref[3:6, 0:CAP] = half_v
@@ -118,6 +118,7 @@
     mig_ref[0] = select_rows(rows, onehot)
     own_ref[0:8, :] = rows
     own_ref[8:9, :] = jnp.where(code == 0.0, rank[0:1, :], -1.0)
+    own_ref[9:10, :] = jnp.broadcast_to(side, (1, PAD))
 
     pl.semaphore_wait(barrier, 7)
     copies = []
@@ -149,8 +150,8 @@
     return [scale * d for d in delta], [well, dist_sq * inv_r, jnp.where(in_range, 1.0, 0.0)]
 
 
-def force_kernel(own_ref, all_ref, mig_ref, side_ref, pos_ref, vel_ref, frc_ref, id_ref, ok_ref, en_ref, cand_ref, near_ref, mine_ref, acc_ref, plane_ref, list_ref):
-    side = side_ref[0, 0]
+def force_kernel(own_ref, all_ref, mig_ref, pos_ref, vel_ref, frc_ref, id_ref, ok_ref, en_ref, cand_ref, near_ref, mine_ref, acc_ref, plane_ref, list_ref):
+    side = own_ref[9:10, 0:1]
     box = side * 2.0
     lane = lax.broadcasted_iota(jnp.int32, (1, MIG), 1)
     arrivals = jnp.zeros((8, MIG), jnp.float32)
@@ -250,14 +251,16 @@
 
         zero = jnp.zeros((8, 128), jnp.float32)
         well, distance, pairs = lax.fori_loop(0, n_own, own_step, (zero,) * 3)
-        energy = 4.0 * well - UPC * distance - (UCUT - RC * UPC) * pairs
+        energy = 2.0 * well - (0.5 * UPC) * distance - (0.5 * (UCUT - RC * UPC)) * pairs
         en_ref[...] = jnp.sum(energy, axis=0, keepdims=True)
 
-    @pl.when(side >= 2.0 * RC)
+    one_image = side[0, 0] >= 2.0 * RC
+
+    @pl.when(one_image)
     def _():
         sweep(None)
 
-    @pl.when(side < 2.0 * RC)
+    @pl.when(jnp.logical_not(one_image))
     def _():
         sweep(box)
 
@@ -288,14 +291,12 @@
         copy.wait()
     parts_ref[0] = en_ref[...]
     over_x = [parts_ref[k] + parts_ref[k + 1] for k in (0, 2, 4, 6)]
-    total = (over_x[0] + over_x[1]) + (over_x[2] + over_x[3])
-    out_ref[...] = jnp.full((1, 1), 0.5 * jnp.sum(total), jnp.float32)
+    out_ref[...] = (over_x[0] + over_x[1]) + (over_x[2] + over_x[3])
 
 
 def solution(mesh):
     vmem = pl.BlockSpec(memory_space=pltpu.VMEM)
     hbm = pl.BlockSpec(memory_space=pltpu.HBM)
-    smem = pl.BlockSpec(memory_space=pltpu.SMEM)
     f32, i32 = jnp.float32, jnp.int32
 
     def shape(dims, dtype=f32):
@@ -303,17 +304,17 @@
 
     exchange = pl.pallas_call(
         exchange_kernel,
-        out_shape=(shape((9, PAD)), shape((8, 1, 3 * PAD)), shape((8, 8, MIG))),
-        in_specs=[hbm] * 5 + [smem],
+        out_shape=(shape((10, PAD)), shape((8, 1, 3 * PAD)), shape((8, 8, MIG))),
+        in_specs=[hbm] * 5 + [pl.BlockSpec(memory_space=pl.ANY)],
         out_specs=(vmem, vmem, vmem),
-        scratch_shapes=[pltpu.VMEM((3, CAP), f32)] * 3 + [pltpu.VMEM((CAP,), i32)] * 2 + [pltpu.VMEM((9, PAD), f32), pltpu.SemaphoreType.DMA((5,)), pltpu.SemaphoreType.DMA((2, 8)), pltpu.SemaphoreType.DMA((2, 8))],
+        scratch_shapes=[pltpu.VMEM((3, CAP), f32)] * 3 + [pltpu.VMEM((CAP,), i32)] * 2 + [pltpu.VMEM((1, 1), f32), pltpu.VMEM((9, PAD), f32), pltpu.SemaphoreType.DMA((6,)), pltpu.SemaphoreType.DMA((2, 8)), pltpu.SemaphoreType.DMA((2, 8))],
         compiler_params=pltpu.CompilerParams(collective_id=0, has_side_effects=True, vmem_limit_bytes=16 << 20),
         name="exchange",
     )
     forces = pl.pallas_call(
         force_kernel,
         out_shape=(shape((3, CAP)), shape((3, CAP)), shape((3, CAP)), shape((CAP,), i32), shape((CAP,), i32), shape((1, 128))),
-        in_specs=[vmem] * 3 + [smem],
+        in_specs=[vmem] * 3,
         out_specs=(vmem,) * 6,
         scratch_shapes=[pltpu.VMEM((8, FULL), f32), pltpu.VMEM((8, 9 * PAD + 256), f32), pltpu.VMEM((3, PAD, 128), f32), pltpu.VMEM((3, PAD, 128), f32), pltpu.VMEM((3, 8, PAD), f32), pltpu.VMEM((8, 8, PAD + 128), f32)],
         compiler_params=pltpu.CompilerParams(vmem_limit_bytes=16 << 20),
@@ -321,7 +322,7 @@
     )
     total_energy = pl.pallas_call(
         energy_kernel,
-        out_shape=shape((1, 1)),
+        out_shape=shape((1, 128)),
         in_specs=[vmem],
         out_specs=vmem,
         scratch_shapes=[pltpu.VMEM((8, 1, 128), f32), pltpu.SemaphoreType.DMA((8,)), pltpu.SemaphoreType.DMA((8,))],
@@ -330,11 +331,11 @@
     )
 
     def local_step(atom_pos, atom_vel, atom_frc, atom_id, atom_ok, brick_side):
-        side = brick_side.reshape(1, 1)
-        own, everyone, movers = exchange(*[pltpu.with_memory_space_constraint(a, pltpu.HBM) for a in (atom_pos.T, atom_vel.T, atom_frc.T, atom_id, atom_ok)], side)
-        pos, vel, frc, new_id, new_ok, partial = forces(own, everyone, movers, side)
-        energy = total_energy(partial)
-        return pos.T, vel.T, frc.T, new_id, new_ok, energy.reshape(())
+        arrays = (atom_pos.T, atom_vel.T, atom_frc.T, atom_id, atom_ok, brick_side.reshape(1, 1))
+        own, everyone, movers = exchange(*[pltpu.with_memory_space_constraint(array, pltpu.HBM) for array in arrays[:5]], arrays[5])
+        pos, vel, frc, new_id, new_ok, partial = forces(own, everyone, movers)
+        energy = jnp.sum(total_energy(partial))
+        return pos.T, vel.T, frc.T, new_id, new_ok, energy
 
     row_spec = P(MESH_AXES, None)
     id_spec = P(MESH_AXES)

time: 23.2 us -> 21 us (0.905)
  between operations: 3.05 us -> 1.3 us
  Pallas kernels: 20.1 us -> 19.1 us
  other arithmetic: 0 us -> 0.6 us
    pallas_call x3, Pallas kernels: 20.1 us -> 19.1 us  [the longest x1 7.61 us: local_step(): exchange(*[pltpu.with_memory_space_constraint(array, pltpu.HBM) for array...]
    reduce_sum x0 -> x1, other arithmetic: none -> 0.6 us  [local_step(): energy = jnp.sum(total_energy(partial))]
where the time goes in v1:
time: 21 us
  Pallas kernels  19.1 us (91%)
  between operations  1.3 us (6%)
  other arithmetic  0.6 us (3%)
    pallas_call x1, Pallas kernels, local_step(): exchange(*[pltpu.with_memory_space_constraint(array, pltpu.HBM) for array...  7.61 us
    pallas_call x1, Pallas kernels, local_step(): pos, vel, frc, new_id, new_ok, partial = forces(own, everyone, movers)  6.18 us
    pallas_call x1, Pallas kernels, local_step(): energy = jnp.sum(total_energy(partial))  5.31 us
    reduce_sum x1, other arithmetic, local_step(): energy = jnp.sum(total_energy(partial))  0.6 us

profile of v1, /device:TPU:0, one launch (start us, length us, event | category | flops | bytes accessed | tf_op | source)
XLA Modules:
  0.0 21.0 jit_solution(17809071831089543266)
XLA Ops:
  1.3 7.6 %exchange.1 = (f32[10,768]{1,0:T(8,128)S(1)}, f32[8,1,2304]{2,1,0:T(1,128)S(1)}, f32[8,8,256]{2,1,0:T(8,128)S(1)}) custom-call(f32[3,729]{1,0:T(4,128)} %bitcast.8, f32[3,729]{1,0:T(4,128)} %bitcast.9, f32[3,729]{1,0:T(4,128)} %bitcast.10, s32[729]{0:T(1024)} %id_hbm.1, s32[729]{0:T(1024)} %ok_hbm.1, f32[1,1]{1,0:T(1,128)} %bitcast.7.side_hbm), custom_call_target="tpu_custom_call" | custom-call | tf_op jit(solution)/shard_map/exchange/pallas_call | solution.py:335
  8.9 6.2 %forces.1 = (f32[3,729]{1,0:T(4,128)}, f32[3,729]{1,0:T(4,128)}, f32[3,729]{1,0:T(4,128)}, s32[729]{0:T(1024)}, s32[729]{0:T(1024)}, /*index=5*/f32[1,128]{1,0:T(1,128)S(1)}) custom-call(f32[10,768]{1,0:T(8,128)S(1)} %get-tuple-element.15.own_ref, f32[8,1,2304]{2,1,0:T(1,128)S(1)} %get-tuple-element.16.all_ref, f32[8,8,256]{2,1,0:T(8,128)S(1)} %get-tuple-element.17.mig_ref), custom_call_target="tpu_custom_call" | custom-call | tf_op jit(solution)/shard_map/forces/pallas_call | solution.py:336
  15.1 5.3 %energy.1 = f32[1,128]{1,0:T(1,128)S(1)} custom-call(f32[1,128]{1,0:T(1,128)S(1)} %get-tuple-element.23.en_ref), custom_call_target="tpu_custom_call" | custom-call | tf_op jit(solution)/shard_map/energy/pallas_call | solution.py:337
  20.4 0.6 %reduce_sum.9 = f32[]{:T(128)} reduce(f32[1,128]{1,0:T(1,128)S(1)} %energy.1, f32[]{:T(128)} %constant.0.clone.1), dimensions={0,1}, to_apply=%region_0.0 | reduce | flops 127 | bytes 520 | tf_op jit(solution)/shard_map/reduce_sum | solution.py:337
